TPU v7x, 32 devices: a whole 2x2x4 slice. The times are simulated.
32 devices in a mesh: parts: 2 (over x), rows: 16 (over z, y, core).
Axes of the slice: x: 2, y: 2, z: 4, core: 2. Of those that a mesh axis runs over, the one named last changes fastest.
Arguments:
- feature_bin: int32 [16384, 700], P(('parts', 'rows')), parts along dimension 0, may hold values from 0 to 255
- doc_leaf: int32 [16384], P(('parts', 'rows')), parts along dimension 0, may hold values from 0 to 31
- current_score: float32 [16384], P(('parts', 'rows')), parts along dimension 0, may hold values from -8 to 8
- relevance: int32 [16384], P(('parts', 'rows')), parts along dimension 0, may hold values from 0 to 4
- doc_rank: int32 [16384], P(('parts', 'rows')), parts along dimension 0, may hold values from 0 to 255, as said below
- query_length: int32 [64], P(('parts', 'rows')), parts along dimension 0, may hold values from 10 to 256, as said below
- feature_votes: int32 [32, 32, 20], P(('parts', 'rows')), parts along dimension 0, may hold values from 0 to 699, all different within a row
- elected: int32 [64, 40], P('parts'), parts along dimension 0, may hold values from 0 to 699, all different within a row
Outputs:
- gradient: float32 [16384], P(('parts', 'rows')), parts along dimension 0
- hessian: float32 [16384], P(('parts', 'rows')), parts along dimension 0
- vote_count: int32 [64, 700], P('parts'), parts along dimension 0
- split_gain: float32 [64, 40, 256], P('parts'), parts along dimension 0
There are 2 independent parts, one for each index of `parts`. A program takes and returns all parts, laid end to end along the dimension named above; each array names one. Nothing has to cross between parts.
Inputs may be any that keep to these rules, and one draw needn't show every extreme that they name: `query_length`: query q holds slots q * 256 to (q + 1) * 256 - 1 of the document arrays; in every draw some query has exactly 256 documents. `doc_rank`: within each query the live documents hold positions 0 to query_length - 1, each once; slots that are not live hold positions from query_length to 255. `feature_votes`: the 20 votes of one device for one leaf are different features. The 40 elected features of one leaf are different.
All inputs are finite; a program needn't handle non-finite values.
Results may differ from a plain program's by a relative error of at most 0.0003.
Values sent between devices are 32-bit elements; how exact they have to be, the bound alone decides.
No kernel may reach another device: no remote copies, remote signals or barrier semaphores. Data moves between devices by JAX's collectives and lax.ppermute only.
A program may use at most 64 MiB of HBM per device.

v0:
```python
import math
import jax
import jax.numpy as jnp
from jax import lax
from jax.sharding import PartitionSpec as P

B = 256
QMAX = 256
ridge_weight = 1.0


def query_terms(scores, levels, places, length):
    positions = jnp.arange(scores.shape[0], dtype=jnp.int32)
    living = positions < length
    gains = jnp.exp2(levels.astype(jnp.float32)) - 1.0
    discount = 1.0 / jnp.log2(places.astype(jnp.float32) + 2.0)
    higher = (levels[None, :] > levels[:, None]) & living[None, :]
    earlier = (
        (levels[None, :] == levels[:, None])
        & (positions[None, :] < positions[:, None])
        & living[None, :]
    )
    ideal_place = jnp.sum((higher | earlier).astype(jnp.float32), axis=1)
    ideal = jnp.sum(jnp.where(living, gains / jnp.log2(ideal_place + 2.0), 0.0))
    scaling = 1.0 / jnp.maximum(ideal, 1.0)
    ordered = (levels[:, None] > levels[None, :]) & living[:, None] & living[None, :]
    chance = jax.nn.sigmoid(scores[None, :] - scores[:, None])
    change = (
        (gains[:, None] - gains[None, :]) * jnp.abs(discount[:, None] - discount[None, :]) * scaling
    )
    pushes = jnp.where(ordered, chance * change, 0.0)
    curves = jnp.where(ordered, chance * (1.0 - chance) * change, 0.0)
    return (
        jnp.sum(pushes, axis=0) - jnp.sum(pushes, axis=1),
        jnp.sum(curves, axis=0) + jnp.sum(curves, axis=1),
    )


def build_histogram(feature_bin, doc_leaf, gradient, hessian, elected, bins):
    leaves, picked = elected.shape
    documents = feature_bin.shape[0]
    leaf_hot = (doc_leaf[:, None] == jnp.arange(leaves, dtype=jnp.int32)[None, :]).astype(
        jnp.float32
    )
    columns = jnp.dot(
        leaf_hot, elected.astype(jnp.float32), precision=lax.Precision.HIGHEST
    ).astype(jnp.int32)
    chosen = jnp.take_along_axis(feature_bin, columns, axis=1)
    weighted = jnp.concatenate([leaf_hot * gradient[:, None], leaf_hot * hessian[:, None]], axis=1)
    block_rows = math.gcd(documents, 512)
    block_count = documents // block_rows
    bin_ids = jnp.arange(bins, dtype=jnp.int32)

    def add_block(index, total):
        onehot = (chosen[:, :, None] == bin_ids[None, None, :]).astype(jnp.float32)
        onehot = onehot.reshape(block_rows, picked * bins)
        return total + jnp.dot(weighted.T, onehot, precision=lax.Precision.HIGHEST)

    empty = jnp.zeros((2 * leaves, picked * bins), jnp.float32)
    total = lax.fori_loop(0, block_count, add_block, empty)
    return total.reshape(2, leaves, picked, bins)


def split_score(prefix, whole):
    remain = whole - prefix
    return (
        prefix[0] * prefix[0] / (prefix[1] + ridge_weight)
        + remain[0] * remain[0] / (remain[1] + ridge_weight)
        - whole[0] * whole[0] / (whole[1] + ridge_weight)
    )


def count_votes(feature_votes, features):
    hits = feature_votes[..., None] == jnp.arange(features, dtype=jnp.int32)
    return jnp.sum(hits.astype(jnp.int32), axis=(0, 2))


def on_device(
    feature_bin, doc_leaf, current_score, relevance, doc_rank, query_length, feature_votes, elected
):
    features = feature_bin.shape[1]
    all_votes = lax.all_gather(feature_votes, "rows", axis=0, tiled=True)
    vote_count = count_votes(all_votes, features)

    def one_query(items):
        return query_terms(items[0], items[1], items[2], items[3])

    gradient, hessian = lax.map(
        one_query,
        (
            current_score.reshape(-1, QMAX),
            relevance.reshape(-1, QMAX),
            doc_rank.reshape(-1, QMAX),
            query_length,
        ),
    )
    gradient = gradient.reshape(-1)
    hessian = hessian.reshape(-1)
    histogram = build_histogram(feature_bin, doc_leaf, gradient, hessian, elected, B)
    summed = lax.psum(histogram, "rows")
    prefix = jnp.cumsum(summed, axis=3)
    whole = jnp.sum(summed, axis=3, keepdims=True)
    split_gain = split_score(prefix, whole)
    return (gradient, hessian, vote_count, split_gain)


def solution(mesh):
    return jax.shard_map(
        on_device,
        mesh=mesh,
        in_specs=(
            P(("parts", "rows"), None),
            P(("parts", "rows")),
            P(("parts", "rows")),
            P(("parts", "rows")),
            P(("parts", "rows")),
            P(("parts", "rows")),
            P(("parts", "rows"), None, None),
            P("parts", None),
        ),
        out_specs=(
            P(("parts", "rows")),
            P(("parts", "rows")),
            P("parts", None),
            P("parts", None, None),
        ),
        check_vma=False,
    )
```

profile of v0, /device:TPU:0, one launch (start us, length us, event | category | flops | bytes accessed | tf_op | source)
XLA Modules:
  0.0 409.0 jit_solution(16073954382203800596)
XLA Ops:
  7.3 0.8 reshape.169
  9.4 9.2 %while.18 = (s32[]{:T(128)}, f32[2,256]{1,0:T(2,128)S(1)}, f32[2,256]{1,0:T(2,128)S(1)}, s32[2,256]{1,0:T(2,128)S(1)}, s32[2]{0:T(128)}, /*index=5*/f32[2,256]{1...) while((s32[]{:T(128)}, f32[2,256]{1,0:T(2,128)S(1)}, f32[2,256]{1,0:T(2,128)S(1)}, ...), condition=%wide.region_7.8_spmd, body=%wide.region_0.7_spmd.sunk | while | flops 2035203 | bytes 32681 | solution.py:88
  9.5 1.2 dynamic_slice.34
  11.6 1.3 exponential_add_fusion.5
  14.1 1.2 dynamic_slice.34
  16.2 1.3 exponential_add_fusion.5
  18.7 1.0 bitcast_or_fusion
  20.0 163.1 %gather_fusion = s32[20480]{0:T(1024)S(1)} fusion(s32[512,700]{0,1:T(8,128)S(1)} %copy-done, s32[20480]{0:T(1024)S(1)} %reshape.179), kind=kCustom, calls=%fused_computation | custom fusion | bytes 327680 | tf_op jit(solution)/shard_map/jit(take_along_axis)/gather | solution.py:48
  183.5 3.3 bitcast_compare_fusion
  186.8 11.0 %fusion.22 = f32[2,32,40,256]{3,1,2,0:T(8,128)} fusion(f32[2,32,512,1]{2,1,3,0:T(8,128)S(1)} %bitcast.69, pred[40,256,512,1]{2,1,0,3:T(32,128)(4,1)S(1)} %bitcast.68), kind=kOutput, calls=%fused_computation.56 | convolution fusion | flops 4026531840 | bytes 7995392 | tf_op jit(solution)/shard_map/while/body/eval_jaxpr/dot_general | solution.py:57
  198.6 24.5 %all_gather.3 = s32[16,32,20]{1,2,0:T(8,128)S(1)} all-gather(s32[1,32,20]{1,2,0:T(8,128)S(1)} %copy.33), channel_id=1, replica_groups=mesh['parts'=2,'rows'=16] {'rows'}, dimensions={0}, use_global_device_ids=true | all-gather | bytes 43520 | tf_op jit(solution)/shard_map/all_gather | solution.py:82
  223.1 4.4 %convert_reduce_fusion.1 = s32[32,700]{1,0:T(8,128)} fusion(s32[16,32,20]{1,2,0:T(8,128)S(1)} %all_gather.3), kind=kLoop, calls=%fused_computation.25 | loop fusion | flops 21481600 | bytes 130560 | tf_op jit(solution)/shard_map/reduce_sum | solution.py:75
  227.5 74.4 %all-reduce.2.cloned.1.call-done = f32[2,32,40,256]{3,1,2,0:T(8,128)} async-done(((f32[2,32,40,256]{3,1,2,0:T(8,128)}), f32[2,32,40,256]{3,1,2,0:T(8,128)}) %all-reduce.2.cloned.1.call-update) | async-done | bytes 2621456 | tf_op jit(solution)/shard_map/psum | solution.py:100
  302.0 2.2 reduce_sum.91
  304.2 4.3 %reshape.175 = f32[2,32,40,2,128]{4,3,1,2,0:T(2,128)} reshape(f32[2,32,40,256]{3,1,2,0:T(8,128)} %all-reduce.2.cloned.1.call-done) | data formatting | bytes 5242880 | tf_op jit(solution)/shard_map/reshape.2
  308.5 4.8 %copy.36 = f32[2,32,40,2,128]{4,2,3,1,0:T(8,128)} copy(f32[2,32,40,2,128]{4,3,1,2,0:T(2,128)} %reshape.175) | data formatting | bytes 5242880 | tf_op jit(solution)/shard_map/reshape.2
  313.3 69.9 %reduce-window.6 = f32[2,32,40,2,128]{4,2,3,1,0:T(8,128)} reduce-window(f32[2,32,40,2,128]{4,2,3,1,0:T(8,128)} %copy.36, f32[]{:T(128)} %constant.79.clone.1), window={size=1x1x1x1x128 pad=0_0x0_0x0_0x0_0x127_0}, to_apply=%region_10.11 | reduce-window | flops 83230720 | bytes 5242884 | tf_op jit(solution)/shard_map/reduce-window
  383.1 4.0 slice.41
  387.1 2.7 copy.37
  390.0 2.3 broadcast_add_fusion
  392.5 2.3 bitcast_subtract_fusion
  395.0 1.7 copy.39
  396.7 2.3 div.58
  399.1 3.1 fusion.12
  (55 shorter events, 6.3 us)
Async XLA Ops:
  7.2 12.8 %copy-start = (s32[512,700]{0,1:T(8,128)S(1)}, s32[512,700]{0,1:T(8,128)}, u32[]{:S(2)}) copy-start(s32[512,700]{0,1:T(8,128)} %param.10) | copy-start | bytes 4300804
  7.2 294.8 %all-reduce.2.cloned.1.call-start = ((), (), s32[]{:S(2)}) async-start(), calls=%async_computation | async-start | bytes 5242880 | tf_op jit(solution)/shard_map/psum | solution.py:100
  18.6 164.8 %copy-start.3 = (f32[1,2,2,128]{3,1,2,0:T(2,128)}, f32[1,2,2,128]{3,1,2,0:T(2,128)S(1)}, u32[]{:S(2)}) copy-start(f32[1,2,2,128]{3,1,2,0:T(2,128)S(1)} %copy.45) | copy-start | bytes 6148
  18.7 164.8 %copy-start.4 = (f32[1,2,2,128]{3,1,2,0:T(2,128)}, f32[1,2,2,128]{3,1,2,0:T(2,128)S(1)}, u32[]{:S(2)}) copy-start(f32[1,2,2,128]{3,1,2,0:T(2,128)S(1)} %copy.46) | copy-start | bytes 6148
  20.0 163.4 %copy-start.5 = (s32[512]{0:T(512)S(1)}, s32[512]{0:T(512)}, u32[]{:S(2)}) copy-start(s32[512]{0:T(512)} %param.11) | copy-start | bytes 6148
  197.9 0.7 copy-start.2
  390.0 2.5 copy-start.1
Sparse Core Ops, SparseCore 0:
  198.0 103.8 all-reduce.1
where the time goes:
time: 417 us; the launch traced here: 409 us
  local copies, waits for them, and re-layouts  189 us (45%)
  other arithmetic  92.9 us (22%)
  waiting for transfers between devices  74.4 us (18%)
  blocking collectives  24.5 us (6%)
  between operations  14.3 us (3%)
  matrix products  12 us (3%)
    gather x5, local copies, waits for them, and re-layouts, build_histogram(): chosen = jnp.take_along_axis(feature_bin, columns, axis=1)  164 us
    psum x1, waiting for transfers between devices, on_device(): summed = lax.psum(histogram, 'rows')  74.4 us
    another operation x5, other arithmetic  72.3 us
    all_gather x1, blocking collectives, on_device(): all_votes = lax.all_gather(feature_votes, 'rows', axis=0, tiled=True)  24.5 us
    dot_general x1, matrix products, add_block(): return total + jnp.dot(weighted.T, onehot, precision=lax.Precision.HIGHEST)  11 us
    another operation x4, local copies, waits for them, and re-layouts  9.1 us
  transfers between devices with their start and end apart: 1, of which 1 were waited for; matrix products, arithmetic and copies ran while one was open for 1% of the time, Pallas kernels for 0%

commit v1 on v0

--- a/solution.py
+++ b/solution.py
@@ -97,7 +97,7 @@
     gradient = gradient.reshape(-1)
     hessian = hessian.reshape(-1)
     histogram = build_histogram(feature_bin, doc_leaf, gradient, hessian, elected, B)
-    summed = lax.psum(histogram, "rows")
+    summed = jnp.sum(lax.all_gather(histogram, "rows"), axis=0)
     prefix = jnp.cumsum(summed, axis=3)
     whole = jnp.sum(summed, axis=3, keepdims=True)
     split_gain = split_score(prefix, whole)

time: 417 us -> 554 us (1.33)
  waiting for transfers between devices: 74.4 us -> 181 us
  other arithmetic: 92.9 us -> 127 us
    all_gather x0 -> x1, waiting for transfers between devices: none -> 181 us  [on_device(): summed = jnp.sum(lax.all_gather(histogram, 'rows'), axis=0)]
    psum x1 -> x0, waiting for transfers between devices: 74.4 us -> none  [on_device(): summed = lax.psum(histogram, 'rows')]
    reduce_sum x0 -> x1, other arithmetic: none -> 16.6 us  [on_device(): summed = jnp.sum(lax.all_gather(histogram, 'rows'), axis=0)]
    reduce_sum x1 -> x2, other arithmetic: 2.15 us -> 16.9 us  [on_device(): whole = jnp.sum(summed, axis=3, keepdims=True)]
    another operation x4 -> x3, local copies, waits for them, and re-layouts: 9.1 us -> 3.54 us
where the time goes in v1:
time: 554 us; the launch traced here: 546 us
  local copies, waits for them, and re-layouts  187 us (34%)
  waiting for transfers between devices  181 us (33%)
  other arithmetic  127 us (23%)
  blocking collectives  24.8 us (4%)
  between operations  14.3 us (3%)
  matrix products  10.5 us (2%)
    all_gather x1, waiting for transfers between devices, on_device(): summed = jnp.sum(lax.all_gather(histogram, 'rows'), axis=0)  181 us
    gather x5, local copies, waits for them, and re-layouts, build_histogram(): chosen = jnp.take_along_axis(feature_bin, columns, axis=1)  164 us
    another operation x5, other arithmetic  71.9 us
    all_gather x1, blocking collectives, on_device(): all_votes = lax.all_gather(feature_votes, 'rows', axis=0, tiled=True)  24.8 us
    reduce_sum x2, other arithmetic, on_device(): whole = jnp.sum(summed, axis=3, keepdims=True)  16.9 us
    reduce_sum x1, other arithmetic, on_device(): summed = jnp.sum(lax.all_gather(histogram, 'rows'), axis=0)  16.6 us
  transfers between devices with their start and end apart: 1, of which 1 were waited for; matrix products, arithmetic and copies ran while one was open for 1% of the time, Pallas kernels for 0%

profile of v1, /device:TPU:0, one launch (start us, length us, event | category | flops | bytes accessed | tf_op | source)
XLA Modules:
  0.0 546.1 jit_solution(1254323526472708985)
XLA Ops:
  9.4 9.2 %while.18 = (s32[]{:T(128)}, f32[2,256]{1,0:T(2,128)S(1)}, f32[2,256]{1,0:T(2,128)S(1)}, s32[2,256]{1,0:T(2,128)S(1)}, s32[2]{0:T(128)}, /*index=5*/f32[2,256]{1...) while((s32[]{:T(128)}, f32[2,256]{1,0:T(2,128)S(1)}, f32[2,256]{1,0:T(2,128)S(1)}, ...), condition=%wide.region_7.8_spmd, body=%wide.region_0.7_spmd.sunk | while | flops 2035203 | bytes 32689 | solution.py:88
  9.4 1.2 dynamic_slice.34
  11.6 1.3 exponential_add_fusion.5
  14.0 1.2 dynamic_slice.34
  16.2 1.3 exponential_add_fusion.5
  20.1 163.1 %gather_fusion = s32[20480]{0:T(1024)S(1)} fusion(s32[512,700]{0,1:T(8,128)S(1)} %copy-done, s32[20480]{0:T(1024)S(1)} %reshape.184), kind=kCustom, calls=%fused_computation | custom fusion | bytes 327680 | tf_op jit(solution)/shard_map/jit(take_along_axis)/gather | solution.py:48
  183.5 3.3 bitcast_compare_fusion
  186.8 9.5 %fusion.21 = f32[2,32,40,256]{3,1,2,0:T(8,128)S(1)} fusion(f32[2,32,512,1]{2,1,3,0:T(8,128)S(1)} %bitcast.77, pred[40,256,512,1]{2,1,0,3:T(32,128)(4,1)S(1)} %bitcast.75), kind=kOutput, calls=%fused_computation.55 | convolution fusion | flops 4026531840 | bytes 7995392 | tf_op jit(solution)/shard_map/while/body/eval_jaxpr/dot_general | solution.py:57
  196.3 3.0 copy.52
  200.1 24.8 %all_gather.6 = s32[16,32,20]{1,2,0:T(8,128)S(1)} all-gather(s32[1,32,20]{1,2,0:T(8,128)S(1)} %copy.49), channel_id=1, replica_groups=mesh['parts'=2,'rows'=16] {'rows'}, dimensions={0}, use_global_device_ids=true | all-gather | bytes 43520 | tf_op jit(solution)/shard_map/all_gather | solution.py:82
  224.9 4.4 convert_reduce_fusion.1
  229.3 181.2 %all-gather.3.cloned.1.call-done = f32[32,32,40,256]{3,2,1,0:T(8,128)} async-done(((f32[2,32,40,256]{3,2,1,0:T(8,128)}), f32[32,32,40,256]{3,2,1,0:T(8,128)}) %all-gather.3.cloned.1.call-update) | async-done | bytes 41943056 | tf_op jit(solution)/shard_map/all_gather | solution.py:100
  410.5 16.6 %reduce_sum.100 = f32[2,32,40,256]{3,2,1,0:T(8,128)} reduce(f32[16,2,32,40,256]{4,3,2,1,0:T(8,128)} %bitcast.74, f32[]{:T(128)} %constant.79.clone.1), dimensions={0}, to_apply=%region_9.10 | reduce | flops 9830400 | bytes 44564484 | tf_op jit(solution)/shard_map/reduce_sum | solution.py:100
  427.1 3.5 copy_bitcast_fusion
  430.6 69.8 %reduce-window.6 = f32[2,32,40,2,128]{4,2,3,1,0:T(8,128)} reduce-window(f32[2,32,40,2,128]{4,2,3,1,0:T(8,128)} %copy_bitcast_fusion, f32[]{:T(128)} %constant.79.clone.1), window={size=1x1x1x1x128 pad=0_0x0_0x0_0x0_0x127_0}, to_apply=%region_10.11 | reduce-window | flops 83230720 | bytes 5242884 | tf_op jit(solution)/shard_map/reduce-window
  500.4 16.9 %reduce.1 = f32[32,32,40]{2,1,0:T(8,128)S(1)} reduce(f32[32,32,40,256]{3,2,1,0:T(8,128)} %all-gather.3.cloned.1.call-done, f32[]{:T(128)} %constant.79.clone.1), dimensions={3}, to_apply=%region_12.13 | reduce | flops 10444800 | bytes 42106884 | tf_op jit(solution)/shard_map/reduce_sum | solution.py:102
  517.3 4.0 slice.41
  521.3 2.7 copy.56
  524.2 3.7 bitcast_subtract_fusion
  528.0 1.9 broadcast_add_fusion
  530.1 1.9 fusion.13
  532.0 1.7 copy.58
  533.8 2.4 div.58
  536.2 3.0 fusion.12
  (61 shorter events, 7.9 us)
Async XLA Ops:
  7.2 12.9 %copy-start = (s32[512,700]{0,1:T(8,128)S(1)}, s32[512,700]{0,1:T(8,128)}, u32[]{:S(2)}) copy-start(s32[512,700]{0,1:T(8,128)} %param.10) | copy-start | bytes 4300804
  7.2 403.4 %all-gather.3.cloned.1.call-start = ((), (), s32[]{:S(2)}) async-start(), calls=%async_computation | async-start | bytes 44564480 | tf_op jit(solution)/shard_map/all_gather | solution.py:100
  18.6 164.8 %copy-start.4 = (f32[1,2,2,128]{3,1,2,0:T(2,128)}, f32[1,2,2,128]{3,1,2,0:T(2,128)S(1)}, u32[]{:S(2)}) copy-start(f32[1,2,2,128]{3,1,2,0:T(2,128)S(1)} %copy.77) | copy-start | bytes 6148
  18.7 164.8 %copy-start.5 = (f32[1,2,2,128]{3,1,2,0:T(2,128)}, f32[1,2,2,128]{3,1,2,0:T(2,128)S(1)}, u32[]{:S(2)}) copy-start(f32[1,2,2,128]{3,1,2,0:T(2,128)S(1)} %copy.76) | copy-start | bytes 6148
  20.0 163.4 %copy-start.6 = (s32[512]{0:T(512)S(1)}, s32[512]{0:T(512)}, u32[]{:S(2)}) copy-start(s32[512]{0:T(512)} %param.11) | copy-start | bytes 6148
  199.4 0.7 copy-start.3
  524.2 3.7 copy-start.2
  533.8 5.5 %copy-start.1 = (s32[512,700]{0,1:T(8,128)S(1)}, s32[512,700]{0,1:T(8,128)}, u32[]{:S(2)}) copy-start(s32[512,700]{0,1:T(8,128)} %param.10) | copy-start | bytes 4300804
Sparse Core Ops, SparseCore 0:
  199.5 210.9 all-gather.2
